TPU v7x, 32 devices: a whole 2x2x4 slice. The times are simulated.
32 devices in a mesh: tensor: 4 (over y, x), dp: 8 (over z, core).
Axes of the slice: x: 2, y: 2, z: 4, core: 2. Of those that a mesh axis runs over, the one named last changes fastest.
Arguments:
- images: bfloat16 [32, 729, 1152], P('dp'), may hold values from -16 to 16
- counts: int32 [8], P('dp'), may hold values from 3 to 4, as said below
- ln1_gain: bfloat16 [1152], replicated, may hold values from 0.099609375 to 1.8984375
- ln1_bias: bfloat16 [1152], replicated, may hold values from -3 to 3
- qkv_weight: bfloat16 [3, 1152, 1152], P(None, None, 'tensor'), may hold values from -1 to 1
- qv_bias: bfloat16 [2, 1152], P(None, 'tensor'), may hold values from -3 to 3
- out_weight: bfloat16 [1152, 1152], P('tensor'), may hold values from -1.5 to 1.5
- out_bias: bfloat16 [1152], replicated, may hold values from -3 to 3
- ln2_gain: bfloat16 [1152], replicated, may hold values from 0.099609375 to 1.8984375
- ln2_bias: bfloat16 [1152], replicated, may hold values from -3 to 3
- fc1_weight: bfloat16 [1152, 4304], P(None, 'tensor'), may hold values from -0.1875 to 0.1875
- fc1_bias: bfloat16 [4304], P('tensor'), may hold values from -3 to 3
- fc2_weight: bfloat16 [4304, 1152], P('tensor'), may hold values from -0.25 to 0.25
- fc2_bias: bfloat16 [1152], replicated, may hold values from -3 to 3
- grad_out: bfloat16 [32, 729, 1152], P('dp'), may hold values from -6 to 6
Outputs:
- block_out: float32 [32, 729, 1152], P('dp', None, 'tensor')
- grad_in: float32 [32, 729, 1152], P('dp', None, 'tensor')
- grad_ln1_gain: float32 [1152], P('tensor')
- grad_ln1_bias: float32 [1152], P('tensor')
- grad_qkv_weight: float32 [3, 1152, 1152], P(None, None, 'tensor')
- grad_qv_bias: float32 [2, 1152], P(None, 'tensor')
- grad_out_weight: float32 [1152, 1152], P('tensor')
- grad_out_bias: float32 [1152], P('tensor')
- grad_ln2_gain: float32 [1152], P('tensor')
- grad_ln2_bias: float32 [1152], P('tensor')
- grad_fc1_weight: float32 [1152, 4304], P(None, 'tensor')
- grad_fc1_bias: float32 [4304], P('tensor')
- grad_fc2_weight: float32 [4304, 1152], P('tensor')
- grad_fc2_bias: float32 [1152], P('tensor')
Inputs may be any that keep to these rules, and one draw needn't show every extreme that they name: `counts`: exactly 6 of the 8 replicas hold 4 live images, the others 4 - 1; a replica's live images fill its first slots.
All inputs are finite; a program needn't handle non-finite values.
Results may differ from a plain program's by a relative error of at most 0.02.
Values may be sent and summed in bfloat16 or wider, within the bound.
A program may use at most 192 MiB of HBM per device.

v0:
```python
import math
import jax
import jax.numpy as jnp
from jax import lax
from jax.sharding import PartitionSpec as P

HD = 72
EPS = 1e-06


def own_columns(values, share_width):
    start = lax.axis_index("tensor") * share_width
    return lax.dynamic_slice_in_dim(values, start, share_width, values.ndim - 1)


def row_mean(values):
    return jnp.mean(values, axis=-1, keepdims=True)


def group_stats(first, second):
    return lax.psum((first, second), "tensor")


def contract_rows(left, right):
    return lax.dot_general(
        left, right, (((0,), (0,)), ((), ())), preferred_element_type=jnp.float32
    )


def contract_cols(left, right):
    return lax.dot_general(
        left, right, (((1,), (1,)), ((), ())), preferred_element_type=jnp.float32
    )


def gelu_tanh(values):
    return jax.nn.gelu(values, approximate=True)


def local(
    images,
    counts,
    ln1_gain,
    ln1_bias,
    qkv_weight,
    qv_bias,
    out_weight,
    out_bias,
    ln2_gain,
    ln2_bias,
    fc1_weight,
    fc1_bias,
    fc2_weight,
    fc2_bias,
    grad_out,
):
    slot_count, length, full_width = images.shape
    share_width = full_width // lax.axis_size("tensor")
    local_width = qkv_weight.shape[2]
    local_heads = local_width // HD
    hidden_width = fc1_weight.shape[1]
    score_scale = 1.0 / math.sqrt(HD)
    gain_one = ln1_gain.astype(jnp.float32)
    shift_one = ln1_bias.astype(jnp.float32)
    gain_two = ln2_gain.astype(jnp.float32)
    shift_two = ln2_bias.astype(jnp.float32)
    bias_out = out_bias.astype(jnp.float32)
    bias_fc1 = fc1_bias.astype(jnp.float32)
    bias_fc2 = fc2_bias.astype(jnp.float32)
    bias_query = qv_bias[0].astype(jnp.float32)
    bias_value = qv_bias[1].astype(jnp.float32)
    live_count = counts[0]

    def to_heads(values):
        return values.reshape(length, local_heads, HD)

    def head_scores(query_heads, key_heads):
        return (
            jnp.einsum("qhd,khd->hqk", query_heads, key_heads, preferred_element_type=jnp.float32)
            * score_scale
        )

    def layer_step(slot_index, loop_state):
        block_acc, input_acc, grads = loop_state
        (
            grad_gain_one,
            grad_shift_one,
            grad_qkv,
            grad_qv,
            grad_out_w,
            grad_out_b,
            grad_gain_two,
            grad_shift_two,
            grad_fc1_w,
            grad_fc1_b,
            grad_fc2_w,
            grad_fc2_b,
        ) = grads
        live_flag = (slot_index < live_count).astype(jnp.float32)
        picture = lax.dynamic_index_in_dim(images, slot_index, 0, keepdims=False).astype(
            jnp.float32
        )
        upstream = (
            lax.dynamic_index_in_dim(grad_out, slot_index, 0, keepdims=False).astype(jnp.float32)
            * live_flag
        )
        upstream_low = upstream.astype(jnp.bfloat16)
        centered = picture - row_mean(picture)
        inv_one = lax.rsqrt(row_mean(centered * centered) + EPS)
        unit_one = centered * inv_one
        normed_one = (unit_one * gain_one + shift_one).astype(jnp.bfloat16)
        query_rows = (
            jnp.dot(normed_one, qkv_weight[0], preferred_element_type=jnp.float32) + bias_query
        ).astype(jnp.bfloat16)
        key_rows = jnp.dot(normed_one, qkv_weight[1], preferred_element_type=jnp.float32).astype(
            jnp.bfloat16
        )
        value_rows = (
            jnp.dot(normed_one, qkv_weight[2], preferred_element_type=jnp.float32) + bias_value
        ).astype(jnp.bfloat16)
        query_heads = to_heads(query_rows)
        key_heads = to_heads(key_rows)
        value_heads = to_heads(value_rows)
        scores = head_scores(query_heads, key_heads)
        row_top = jnp.max(scores, axis=-1, keepdims=True)
        logsum = row_top + jnp.log(jnp.sum(jnp.exp(scores - row_top), axis=-1, keepdims=True))
        probs_low = jnp.exp(scores - logsum).astype(jnp.bfloat16)
        mixed = jnp.einsum(
            "hqk,khd->qhd", probs_low, value_heads, preferred_element_type=jnp.float32
        )
        mixed = mixed.reshape(length, local_width).astype(jnp.bfloat16)
        partial_out = jnp.dot(mixed, out_weight, preferred_element_type=jnp.float32).astype(
            jnp.bfloat16
        )
        residual = (
            own_columns(picture, share_width)
            + lax.psum_scatter(partial_out, "tensor", scatter_dimension=1, tiled=True).astype(
                jnp.float32
            )
            + own_columns(bias_out, share_width)
        )
        row_sum, row_square = group_stats(
            jnp.sum(residual, axis=-1), jnp.sum(residual * residual, axis=-1)
        )
        average = row_sum[:, None] / full_width
        inv_two = lax.rsqrt(row_square[:, None] / full_width - average * average + EPS)
        unit_two = (residual - average) * inv_two
        own_normed = (
            unit_two * own_columns(gain_two, share_width) + own_columns(shift_two, share_width)
        ).astype(jnp.bfloat16)
        normed_two = lax.all_gather(own_normed, "tensor", axis=1, tiled=True)
        preact = jnp.dot(normed_two, fc1_weight, preferred_element_type=jnp.float32) + bias_fc1
        activated = gelu_tanh(preact).astype(jnp.bfloat16)
        partial_mlp = jnp.dot(activated, fc2_weight, preferred_element_type=jnp.float32).astype(
            jnp.bfloat16
        )
        block_rows = (
            residual
            + lax.psum_scatter(partial_mlp, "tensor", scatter_dimension=1, tiled=True).astype(
                jnp.float32
            )
            + own_columns(bias_fc2, share_width)
        )
        block_rows = block_rows * live_flag
        grad_fc2_b = grad_fc2_b + own_columns(jnp.sum(upstream, axis=0), share_width)
        grad_fc2_w = grad_fc2_w + contract_rows(activated, upstream_low)
        d_act = contract_cols(upstream_low, fc2_weight)
        gelu_pull = jax.vjp(gelu_tanh, preact)[1]
        d_pre = gelu_pull(d_act)[0].astype(jnp.bfloat16)
        grad_fc1_b = grad_fc1_b + jnp.sum(d_pre.astype(jnp.float32), axis=0)
        grad_fc1_w = grad_fc1_w + contract_rows(normed_two, d_pre)
        back_mlp = contract_cols(d_pre, fc1_weight)
        d_norm_two = lax.psum_scatter(
            back_mlp.astype(jnp.bfloat16), "tensor", scatter_dimension=1, tiled=True
        ).astype(jnp.float32)
        scaled_two = d_norm_two * own_columns(gain_two, share_width)
        sum_plain, sum_cross = group_stats(
            jnp.sum(scaled_two, axis=-1), jnp.sum(scaled_two * unit_two, axis=-1)
        )
        d_residual = own_columns(upstream, share_width) + inv_two * (
            scaled_two
            - sum_plain[:, None] / full_width
            - unit_two * (sum_cross[:, None] / full_width)
        )
        grad_gain_two = grad_gain_two + jnp.sum(d_norm_two * unit_two, axis=0)
        grad_shift_two = grad_shift_two + jnp.sum(d_norm_two, axis=0)
        grad_out_b = grad_out_b + jnp.sum(d_residual, axis=0)
        d_residual_low = lax.all_gather(
            d_residual.astype(jnp.bfloat16), "tensor", axis=1, tiled=True
        )
        grad_out_w = grad_out_w + contract_rows(mixed, d_residual_low)
        d_mixed_heads = to_heads(contract_cols(d_residual_low, out_weight).astype(jnp.bfloat16))
        probs = jnp.exp(head_scores(query_heads, key_heads) - logsum)
        probs_again = probs.astype(jnp.bfloat16)
        d_value = jnp.einsum(
            "hqk,qhd->khd", probs_again, d_mixed_heads, preferred_element_type=jnp.float32
        )
        d_probs = jnp.einsum(
            "qhd,khd->hqk", d_mixed_heads, value_heads, preferred_element_type=jnp.float32
        )
        inner = jnp.sum(probs * d_probs, axis=-1, keepdims=True)
        d_scores = (probs * (d_probs - inner)).astype(jnp.bfloat16)
        d_query = (
            jnp.einsum("hqk,khd->qhd", d_scores, key_heads, preferred_element_type=jnp.float32)
            * score_scale
        )
        d_key = (
            jnp.einsum("hqk,qhd->khd", d_scores, query_heads, preferred_element_type=jnp.float32)
            * score_scale
        )
        d_stack = (
            jnp.stack([d_query, d_key, d_value], axis=1)
            .reshape(length, 3, local_width)
            .astype(jnp.bfloat16)
        )
        grad_qkv = grad_qkv + jnp.einsum(
            "ld,lje->jde", normed_one, d_stack, preferred_element_type=jnp.float32
        )
        bias_sums = jnp.sum(d_stack.astype(jnp.float32), axis=0)
        grad_qv = grad_qv + jnp.stack([bias_sums[0], bias_sums[2]])
        back_attn = jnp.einsum(
            "lje,jde->ld", d_stack, qkv_weight, preferred_element_type=jnp.float32
        )
        d_norm_one = lax.psum_scatter(
            back_attn.astype(jnp.bfloat16), "tensor", scatter_dimension=1, tiled=True
        ).astype(jnp.float32)
        own_unit = own_columns(unit_one, share_width)
        scaled_one = d_norm_one * own_columns(gain_one, share_width)
        plain_one, cross_one = group_stats(
            jnp.sum(scaled_one, axis=-1), jnp.sum(scaled_one * own_unit, axis=-1)
        )
        d_input = d_residual + inv_one * (
            scaled_one
            - plain_one[:, None] / full_width
            - own_unit * (cross_one[:, None] / full_width)
        )
        grad_gain_one = grad_gain_one + jnp.sum(d_norm_one * own_unit, axis=0)
        grad_shift_one = grad_shift_one + jnp.sum(d_norm_one, axis=0)
        block_acc = lax.dynamic_update_index_in_dim(block_acc, block_rows, slot_index, 0)
        input_acc = lax.dynamic_update_index_in_dim(input_acc, d_input, slot_index, 0)
        new_grads = (
            grad_gain_one,
            grad_shift_one,
            grad_qkv,
            grad_qv,
            grad_out_w,
            grad_out_b,
            grad_gain_two,
            grad_shift_two,
            grad_fc1_w,
            grad_fc1_b,
            grad_fc2_w,
            grad_fc2_b,
        )
        return (block_acc, input_acc, new_grads)

    share_zeros = jnp.zeros((share_width,), jnp.float32)
    start_grads = (
        share_zeros,
        share_zeros,
        jnp.zeros((3, full_width, local_width), jnp.float32),
        jnp.zeros((2, local_width), jnp.float32),
        jnp.zeros((local_width, full_width), jnp.float32),
        share_zeros,
        share_zeros,
        share_zeros,
        jnp.zeros((full_width, hidden_width), jnp.float32),
        jnp.zeros((hidden_width,), jnp.float32),
        jnp.zeros((hidden_width, full_width), jnp.float32),
        share_zeros,
    )
    start_rows = jnp.zeros((slot_count, length, share_width), jnp.float32)
    block_acc, input_acc, grads = lax.fori_loop(
        0, slot_count, layer_step, (start_rows, start_rows, start_grads)
    )
    (
        grad_gain_one,
        grad_shift_one,
        grad_qkv,
        grad_qv,
        grad_out_w,
        grad_out_b,
        grad_gain_two,
        grad_shift_two,
        grad_fc1_w,
        grad_fc1_b,
        grad_fc2_w,
        grad_fc2_b,
    ) = grads
    summed = (
        lax.psum(grad_gain_one.astype(jnp.bfloat16), "dp").astype(jnp.float32),
        lax.psum(grad_shift_one.astype(jnp.bfloat16), "dp").astype(jnp.float32),
        lax.psum(grad_qkv.astype(jnp.bfloat16), "dp").astype(jnp.float32),
        lax.psum(grad_qv.astype(jnp.bfloat16), "dp").astype(jnp.float32),
        lax.psum(grad_out_w.astype(jnp.bfloat16), "dp").astype(jnp.float32),
        lax.psum(grad_out_b.astype(jnp.bfloat16), "dp").astype(jnp.float32),
        lax.psum(grad_gain_two.astype(jnp.bfloat16), "dp").astype(jnp.float32),
        lax.psum(grad_shift_two.astype(jnp.bfloat16), "dp").astype(jnp.float32),
        lax.psum(grad_fc1_w.astype(jnp.bfloat16), "dp").astype(jnp.float32),
        lax.psum(grad_fc1_b.astype(jnp.bfloat16), "dp").astype(jnp.float32),
        lax.psum(grad_fc2_w.astype(jnp.bfloat16), "dp").astype(jnp.float32),
        lax.psum(grad_fc2_b.astype(jnp.bfloat16), "dp").astype(jnp.float32),
    )
    return (
        block_acc,
        input_acc,
        summed[0],
        summed[1],
        summed[2],
        summed[3],
        summed[4],
        summed[5],
        summed[6],
        summed[7],
        summed[8],
        summed[9],
        summed[10],
        summed[11],
    )


def solution(mesh):
    return jax.shard_map(
        local,
        mesh=mesh,
        in_specs=(
            P("dp", None, None),
            P("dp"),
            P(),
            P(),
            P(None, None, "tensor"),
            P(None, "tensor"),
            P("tensor", None),
            P(),
            P(),
            P(),
            P(None, "tensor"),
            P("tensor"),
            P("tensor", None),
            P(),
            P("dp", None, None),
        ),
        out_specs=(
            P("dp", None, "tensor"),
            P("dp", None, "tensor"),
            P("tensor"),
            P("tensor"),
            P(None, None, "tensor"),
            P(None, "tensor"),
            P("tensor", None),
            P("tensor"),
            P("tensor"),
            P("tensor"),
            P(None, "tensor"),
            P("tensor"),
            P("tensor", None),
            P("tensor"),
        ),
        check_vma=False,
    )
```

profile of v0, /device:TPU:0, one launch (start us, length us, event | category | flops | bytes accessed | tf_op | source)
XLA Modules:
  0.0 1362.5 jit_solution(6711157673283328373)
XLA Ops:
  16.7 12.7 copy.34
  29.4 12.7 copy.35
  42.1 1129.5 %while.42 = (s32[]{:T(128)}, f32[4,729,288]{1,2,0:T(8,128)}, f32[4,729,288]{1,2,0:T(8,128)}, f32[288]{0:T(512)}, f32[288]{0:T(512)}, /*index=5*/f32[3,1152,288]{...) while((s32[]{:T(128)}, f32[4,729,288]{1,2,0:T(8,128)}, ...), condition=%wide.region_30.31_spmd.clone, body=%wide.region_0.30_spmd.clone.sunk | while | flops 18614964224 | bytes 394633504 | solution.py:273
  70.5 29.5 %reduce-scatter.5.cloned.1.call-done = bf16[729,288]{0,1:T(8,128)(2,1)} async-done(((bf16[729,1152]{0,1:T(8,128)(2,1)}), bf16[729,288]{0,1:T(8,128)(2,1)}) %reduce-scatter.5.cloned.1.call-update) | async-done | bytes 419920 | tf_op jit(solution)/shard_map/while/body/eval_jaxpr/reduce_scatter | solution.py:137
  101.5 9.1 all-reduce.8
  112.9 31.3 %all-gather.3.cloned.1.call-done = bf16[729,1152]{0,1:T(8,128)(2,1)} async-done(((bf16[729,288]{0,1:T(8,128)(2,1)}), bf16[729,1152]{0,1:T(8,128)(2,1)}) %all-gather.3.cloned.1.call-update) | async-done | bytes 1679632 | tf_op jit(solution)/shard_map/while/body/eval_jaxpr/all_gather | solution.py:151
  149.0 7.7 convert_reduce_fusion.11
  165.4 29.0 %reduce-scatter.9.cloned.1.call-done = bf16[729,288]{0,1:T(8,128)(2,1)} async-done(((bf16[729,1152]{0,1:T(8,128)(2,1)}), bf16[729,288]{0,1:T(8,128)(2,1)}) %reduce-scatter.9.cloned.1.call-update) | async-done | bytes 419920 | tf_op jit(solution)/shard_map/while/body/eval_jaxpr/reduce_scatter | solution.py:173
  196.4 9.1 all-reduce.9
  215.2 6.1 convolution_convert_fusion.17
  221.4 19.9 %all-gather.5.cloned.1.call-done = bf16[729,1152]{0,1:T(8,128)(2,1)} async-done(((bf16[729,288]{0,1:T(8,128)(2,1)}), bf16[729,1152]{0,1:T(8,128)(2,1)}) %all-gather.5.cloned.1.call-update) | async-done | bytes 1679632 | tf_op jit(solution)/shard_map/while/body/eval_jaxpr/all_gather | solution.py:188
  243.7 7.6 multiply_reduce_fusion.9
  251.3 10.4 multiply_convert_fusion.9
  266.8 5.7 convolution_convert_fusion.20
  278.1 6.8 convolution_add_fusion.12
  285.5 6.9 convolution_add_fusion.13
  299.2 6.0 bitcast_add_fusion.3
  305.2 6.9 reduce-scatter.11.cloned.1.call-done
  313.8 9.1 all-reduce.10
  354.3 26.8 %reduce-scatter.5.cloned.1.call-done = bf16[729,288]{0,1:T(8,128)(2,1)} async-done(((bf16[729,1152]{0,1:T(8,128)(2,1)}), bf16[729,288]{0,1:T(8,128)(2,1)}) %reduce-scatter.5.cloned.1.call-update) | async-done | bytes 419920 | tf_op jit(solution)/shard_map/while/body/eval_jaxpr/reduce_scatter | solution.py:137
  382.6 9.1 all-reduce.8
  393.6 31.7 %all-gather.3.cloned.1.call-done = bf16[729,1152]{0,1:T(8,128)(2,1)} async-done(((bf16[729,288]{0,1:T(8,128)(2,1)}), bf16[729,1152]{0,1:T(8,128)(2,1)}) %all-gather.3.cloned.1.call-update) | async-done | bytes 1679632 | tf_op jit(solution)/shard_map/while/body/eval_jaxpr/all_gather | solution.py:151
  430.1 7.7 convert_reduce_fusion.11
  446.5 29.0 %reduce-scatter.9.cloned.1.call-done = bf16[729,288]{0,1:T(8,128)(2,1)} async-done(((bf16[729,1152]{0,1:T(8,128)(2,1)}), bf16[729,288]{0,1:T(8,128)(2,1)}) %reduce-scatter.9.cloned.1.call-update) | async-done | bytes 419920 | tf_op jit(solution)/shard_map/while/body/eval_jaxpr/reduce_scatter | solution.py:173
  477.4 9.1 all-reduce.9
  496.9 6.1 convolution_convert_fusion.17
  503.1 19.2 %all-gather.5.cloned.1.call-done = bf16[729,1152]{0,1:T(8,128)(2,1)} async-done(((bf16[729,288]{0,1:T(8,128)(2,1)}), bf16[729,1152]{0,1:T(8,128)(2,1)}) %all-gather.5.cloned.1.call-update) | async-done | bytes 1679632 | tf_op jit(solution)/shard_map/while/body/eval_jaxpr/all_gather | solution.py:188
  524.8 7.6 multiply_reduce_fusion.9
  532.4 10.3 multiply_convert_fusion.9
  559.2 8.2 convolution_add_fusion.12
  568.1 8.4 convolution_add_fusion.13
  584.7 7.2 bitcast_add_fusion.3
  595.1 9.1 all-reduce.10
  635.3 26.8 %reduce-scatter.5.cloned.1.call-done = bf16[729,288]{0,1:T(8,128)(2,1)} async-done(((bf16[729,1152]{0,1:T(8,128)(2,1)}), bf16[729,288]{0,1:T(8,128)(2,1)}) %reduce-scatter.5.cloned.1.call-update) | async-done | bytes 419920 | tf_op jit(solution)/shard_map/while/body/eval_jaxpr/reduce_scatter | solution.py:137
  663.6 9.1 all-reduce.8
  674.9 31.5 %all-gather.3.cloned.1.call-done = bf16[729,1152]{0,1:T(8,128)(2,1)} async-done(((bf16[729,288]{0,1:T(8,128)(2,1)}), bf16[729,1152]{0,1:T(8,128)(2,1)}) %all-gather.3.cloned.1.call-update) | async-done | bytes 1679632 | tf_op jit(solution)/shard_map/while/body/eval_jaxpr/all_gather | solution.py:151
  711.1 7.7 convert_reduce_fusion.11
  727.5 29.0 %reduce-scatter.9.cloned.1.call-done = bf16[729,288]{0,1:T(8,128)(2,1)} async-done(((bf16[729,1152]{0,1:T(8,128)(2,1)}), bf16[729,288]{0,1:T(8,128)(2,1)}) %reduce-scatter.9.cloned.1.call-update) | async-done | bytes 419920 | tf_op jit(solution)/shard_map/while/body/eval_jaxpr/reduce_scatter | solution.py:173
  758.5 9.1 all-reduce.9
  778.0 6.1 convolution_convert_fusion.17
  784.2 19.2 %all-gather.5.cloned.1.call-done = bf16[729,1152]{0,1:T(8,128)(2,1)} async-done(((bf16[729,288]{0,1:T(8,128)(2,1)}), bf16[729,1152]{0,1:T(8,128)(2,1)}) %all-gather.5.cloned.1.call-update) | async-done | bytes 1679632 | tf_op jit(solution)/shard_map/while/body/eval_jaxpr/all_gather | solution.py:188
  805.8 7.6 multiply_reduce_fusion.9
  813.4 10.4 multiply_convert_fusion.9
  828.9 5.7 convolution_convert_fusion.20
  840.3 8.2 convolution_add_fusion.12
  849.1 8.2 convolution_add_fusion.13
  865.5 7.2 bitcast_add_fusion.3
  875.9 9.1 all-reduce.10
  916.5 26.8 %reduce-scatter.5.cloned.1.call-done = bf16[729,288]{0,1:T(8,128)(2,1)} async-done(((bf16[729,1152]{0,1:T(8,128)(2,1)}), bf16[729,288]{0,1:T(8,128)(2,1)}) %reduce-scatter.5.cloned.1.call-update) | async-done | bytes 419920 | tf_op jit(solution)/shard_map/while/body/eval_jaxpr/reduce_scatter | solution.py:137
  944.8 9.1 all-reduce.8
  955.7 31.7 %all-gather.3.cloned.1.call-done = bf16[729,1152]{0,1:T(8,128)(2,1)} async-done(((bf16[729,288]{0,1:T(8,128)(2,1)}), bf16[729,1152]{0,1:T(8,128)(2,1)}) %all-gather.3.cloned.1.call-update) | async-done | bytes 1679632 | tf_op jit(solution)/shard_map/while/body/eval_jaxpr/all_gather | solution.py:151
  992.2 7.7 convert_reduce_fusion.11
  1008.6 29.0 %reduce-scatter.9.cloned.1.call-done = bf16[729,288]{0,1:T(8,128)(2,1)} async-done(((bf16[729,1152]{0,1:T(8,128)(2,1)}), bf16[729,288]{0,1:T(8,128)(2,1)}) %reduce-scatter.9.cloned.1.call-update) | async-done | bytes 419920 | tf_op jit(solution)/shard_map/while/body/eval_jaxpr/reduce_scatter | solution.py:173
  1039.6 9.1 all-reduce.9
  1059.1 6.1 convolution_convert_fusion.17
  1065.3 19.2 %all-gather.5.cloned.1.call-done = bf16[729,1152]{0,1:T(8,128)(2,1)} async-done(((bf16[729,288]{0,1:T(8,128)(2,1)}), bf16[729,1152]{0,1:T(8,128)(2,1)}) %all-gather.5.cloned.1.call-update) | async-done | bytes 1679632 | tf_op jit(solution)/shard_map/while/body/eval_jaxpr/all_gather | solution.py:188
  1086.9 7.6 multiply_reduce_fusion.9
  1094.5 10.3 multiply_convert_fusion.9
  1121.4 8.2 convolution_add_fusion.12
  1130.3 8.4 convolution_add_fusion.13
  1146.8 7.2 bitcast_add_fusion.3
  1157.2 9.1 all-reduce.10
  1184.1 27.8 %all-reduce.3 = (bf16[288]{0:T(512)(128)(2,1)S(1)}, bf16[288]{0:T(512)(128)(2,1)S(1)}, bf16[2,288]{1,0:T(2,128)(2,1)S(1)}, bf16[288]{0:T(512)(128)(2,1)S(1)}, bf...) all-reduce(bf16[288]{0:T(512)(128)(2,1)S(1)} %convert_element_type., ...), channel_id=1, replica_groups=mesh['tensor'=4,'dp'=8] {'dp'}, use_global_device_ids=true, to_apply=%region_31.32 | all-reduce | flops 3380 | bytes 13520 | tf_op jit(solution)/shard_map/psum | solution.py:291
  1216.5 127.7 %all-reduce.13.cloned.1.call-done = (bf16[3,1152,288]{1,2,0:T(8,128)(2,1)}, bf16[288,1152]{1,0:T(8,128)(2,1)}, bf16[1152,1076]{0,1:T(8,128)(2,1)}, bf16[1076,1152]{1,0:T(8,128)(2,1)}) async-done(((bf16[3,1152,288]{1,2,0:T(8,128)(2,1)}, bf16[288,1152]{1,0:T(8,128)(2,1)}, bf16[1152,1076]{0,1:T(8,128)(2,1)}, bf16[1076,1152]{1,0:T(8,128)(2,1)}), (bf16[3,1152,288]{1,2,0:T(8,128)(2,1)}, ...) | async-done | bytes 7612432 | tf_op jit(solution)/shard_map/psum | solution.py:293
  (640 shorter events, 382.3 us)
Async XLA Ops:
  42.1 9.8 copy-start.41
  42.1 166.6 %copy-start.18 = (f32[1152]{0:T(1024)}, f32[1152]{0:T(1024)S(1)}, u32[]{:S(2)}) copy-start(f32[1152]{0:T(1024)S(1)} %get-tuple-element.1334) | copy-start | bytes 13828 | tf_op jit(solution)/shard_map/while
  42.1 57.8 %reduce-scatter.5.cloned.1.call-start = ((), (), s32[]{:S(2)}) async-start(), calls=%async_computation.5 | async-start | bytes 2211840 | tf_op jit(solution)/shard_map/while/body/eval_jaxpr/reduce_scatter | solution.py:137
  44.0 167.6 %copy-start.15 = (f32[729]{0:T(1024)}, f32[729]{0:T(1024)S(1)}, u32[]{:S(2)}) copy-start(f32[729]{0:T(1024)S(1)} %broadcast_multiply_fusion.11) | copy-start | bytes 8752 | tf_op jit(solution)/shard_map/while
  64.6 79.6 %all-gather.3.cloned.1.call-start = ((), (), s32[]{:S(2)}) async-start(), calls=%async_computation.6 | async-start | bytes 2211840 | tf_op jit(solution)/shard_map/while/body/eval_jaxpr/all_gather | solution.py:151
  111.6 82.7 %reduce-scatter.9.cloned.1.call-start = ((), (), s32[]{:S(2)}) async-start(), calls=%async_computation.8 | async-start | bytes 2211840 | tf_op jit(solution)/shard_map/while/body/eval_jaxpr/reduce_scatter | solution.py:173
  161.7 79.5 %all-gather.5.cloned.1.call-start = ((), (), s32[]{:S(2)}) async-start(), calls=%async_computation.9 | async-start | bytes 2211840 | tf_op jit(solution)/shard_map/while/body/eval_jaxpr/all_gather | solution.py:188
  208.7 84.9 %reduce-scatter.7.cloned.1.call-start = ((), (), s32[]{:S(2)}) async-start(), calls=%async_computation.7 | async-start | bytes 2211840 | tf_op jit(solution)/shard_map/while/body/eval_jaxpr/reduce_scatter | solution.py:159
  221.3 90.8 %reduce-scatter.11.cloned.1.call-start = ((), (), s32[]{:S(2)}) async-start(), calls=%async_computation.10 | async-start | bytes 2211840 | tf_op jit(solution)/shard_map/while/body/eval_jaxpr/reduce_scatter | solution.py:224
  299.2 12.9 copy-start.17
  299.2 23.7 %copy-start.30 = (f32[288]{0:T(512)S(1)}, f32[288]{0:T(512)}, u32[]{:S(2)}) copy-start(f32[288]{0:T(512)} %get-tuple-element.1286) | copy-start | bytes 3460 | tf_op jit(solution)/shard_map/while
  299.2 23.7 %copy-start.33 = (f32[288]{0:T(512)S(1)}, f32[288]{0:T(512)}, u32[]{:S(2)}) copy-start(f32[288]{0:T(512)} %get-tuple-element.1285) | copy-start | bytes 3460 | tf_op jit(solution)/shard_map/while
  312.1 13.4 copy-start.19
  312.1 13.4 copy-start.21
  312.1 13.4 copy-start.40
  312.1 13.4 copy-start.42
  325.9 9.8 copy-start.41
  325.9 163.9 %copy-start.18 = (f32[1152]{0:T(1024)}, f32[1152]{0:T(1024)S(1)}, u32[]{:S(2)}) copy-start(f32[1152]{0:T(1024)S(1)} %get-tuple-element.1334) | copy-start | bytes 13828 | tf_op jit(solution)/shard_map/while
  325.9 55.1 %reduce-scatter.5.cloned.1.call-start = ((), (), s32[]{:S(2)}) async-start(), calls=%async_computation.5 | async-start | bytes 2211840 | tf_op jit(solution)/shard_map/while/body/eval_jaxpr/reduce_scatter | solution.py:137
  327.8 165.5 %copy-start.15 = (f32[729]{0:T(1024)}, f32[729]{0:T(1024)S(1)}, u32[]{:S(2)}) copy-start(f32[729]{0:T(1024)S(1)} %broadcast_multiply_fusion.11) | copy-start | bytes 8752 | tf_op jit(solution)/shard_map/while
  348.4 76.9 %all-gather.3.cloned.1.call-start = ((), (), s32[]{:S(2)}) async-start(), calls=%async_computation.6 | async-start | bytes 2211840 | tf_op jit(solution)/shard_map/while/body/eval_jaxpr/all_gather | solution.py:151
  392.7 82.7 %reduce-scatter.9.cloned.1.call-start = ((), (), s32[]{:S(2)}) async-start(), calls=%async_computation.8 | async-start | bytes 2211840 | tf_op jit(solution)/shard_map/while/body/eval_jaxpr/reduce_scatter | solution.py:173
  442.8 79.6 %all-gather.5.cloned.1.call-start = ((), (), s32[]{:S(2)}) async-start(), calls=%async_computation.9 | async-start | bytes 2211840 | tf_op jit(solution)/shard_map/while/body/eval_jaxpr/all_gather | solution.py:188
  489.8 88.6 %reduce-scatter.7.cloned.1.call-start = ((), (), s32[]{:S(2)}) async-start(), calls=%async_computation.7 | async-start | bytes 2211840 | tf_op jit(solution)/shard_map/while/body/eval_jaxpr/reduce_scatter | solution.py:159
  503.1 90.2 %reduce-scatter.11.cloned.1.call-start = ((), (), s32[]{:S(2)}) async-start(), calls=%async_computation.10 | async-start | bytes 2211840 | tf_op jit(solution)/shard_map/while/body/eval_jaxpr/reduce_scatter | solution.py:224
  568.1 9.0 copy-start.25
  584.6 19.5 %copy-start.30 = (f32[288]{0:T(512)S(1)}, f32[288]{0:T(512)}, u32[]{:S(2)}) copy-start(f32[288]{0:T(512)} %get-tuple-element.1286) | copy-start | bytes 3460 | tf_op jit(solution)/shard_map/while
  584.6 19.5 %copy-start.33 = (f32[288]{0:T(512)S(1)}, f32[288]{0:T(512)}, u32[]{:S(2)}) copy-start(f32[288]{0:T(512)} %get-tuple-element.1285) | copy-start | bytes 3460 | tf_op jit(solution)/shard_map/while
  593.3 13.4 copy-start.19
  593.3 13.4 copy-start.21
  593.3 13.4 copy-start.40
  593.4 13.4 copy-start.42
  607.0 9.8 copy-start.41
  607.0 163.9 %copy-start.18 = (f32[1152]{0:T(1024)}, f32[1152]{0:T(1024)S(1)}, u32[]{:S(2)}) copy-start(f32[1152]{0:T(1024)S(1)} %get-tuple-element.1334) | copy-start | bytes 13828 | tf_op jit(solution)/shard_map/while
  607.0 55.1 %reduce-scatter.5.cloned.1.call-start = ((), (), s32[]{:S(2)}) async-start(), calls=%async_computation.5 | async-start | bytes 2211840 | tf_op jit(solution)/shard_map/while/body/eval_jaxpr/reduce_scatter | solution.py:137
  608.9 165.5 %copy-start.15 = (f32[729]{0:T(1024)}, f32[729]{0:T(1024)S(1)}, u32[]{:S(2)}) copy-start(f32[729]{0:T(1024)S(1)} %broadcast_multiply_fusion.11) | copy-start | bytes 8752 | tf_op jit(solution)/shard_map/while
  629.5 76.9 %all-gather.3.cloned.1.call-start = ((), (), s32[]{:S(2)}) async-start(), calls=%async_computation.6 | async-start | bytes 2211840 | tf_op jit(solution)/shard_map/while/body/eval_jaxpr/all_gather | solution.py:151
  673.8 82.7 %reduce-scatter.9.cloned.1.call-start = ((), (), s32[]{:S(2)}) async-start(), calls=%async_computation.8 | async-start | bytes 2211840 | tf_op jit(solution)/shard_map/while/body/eval_jaxpr/reduce_scatter | solution.py:173
  723.9 79.6 %all-gather.5.cloned.1.call-start = ((), (), s32[]{:S(2)}) async-start(), calls=%async_computation.9 | async-start | bytes 2211840 | tf_op jit(solution)/shard_map/while/body/eval_jaxpr/all_gather | solution.py:188
  770.8 88.4 %reduce-scatter.7.cloned.1.call-start = ((), (), s32[]{:S(2)}) async-start(), calls=%async_computation.7 | async-start | bytes 2211840 | tf_op jit(solution)/shard_map/while/body/eval_jaxpr/reduce_scatter | solution.py:159
  784.1 90.1 %reduce-scatter.11.cloned.1.call-start = ((), (), s32[]{:S(2)}) async-start(), calls=%async_computation.10 | async-start | bytes 2211840 | tf_op jit(solution)/shard_map/while/body/eval_jaxpr/reduce_scatter | solution.py:224
  865.5 19.6 %copy-start.30 = (f32[288]{0:T(512)S(1)}, f32[288]{0:T(512)}, u32[]{:S(2)}) copy-start(f32[288]{0:T(512)} %get-tuple-element.1286) | copy-start | bytes 3460 | tf_op jit(solution)/shard_map/while
  865.5 19.6 %copy-start.33 = (f32[288]{0:T(512)S(1)}, f32[288]{0:T(512)}, u32[]{:S(2)}) copy-start(f32[288]{0:T(512)} %get-tuple-element.1285) | copy-start | bytes 3460 | tf_op jit(solution)/shard_map/while
  874.2 13.4 copy-start.19
  874.2 13.4 copy-start.21
  874.2 13.4 copy-start.40
  874.2 13.4 copy-start.42
  888.1 9.8 copy-start.41
  888.1 163.9 %copy-start.18 = (f32[1152]{0:T(1024)}, f32[1152]{0:T(1024)S(1)}, u32[]{:S(2)}) copy-start(f32[1152]{0:T(1024)S(1)} %get-tuple-element.1334) | copy-start | bytes 13828 | tf_op jit(solution)/shard_map/while
  888.1 55.1 %reduce-scatter.5.cloned.1.call-start = ((), (), s32[]{:S(2)}) async-start(), calls=%async_computation.5 | async-start | bytes 2211840 | tf_op jit(solution)/shard_map/while/body/eval_jaxpr/reduce_scatter | solution.py:137
  890.0 165.5 %copy-start.15 = (f32[729]{0:T(1024)}, f32[729]{0:T(1024)S(1)}, u32[]{:S(2)}) copy-start(f32[729]{0:T(1024)S(1)} %broadcast_multiply_fusion.11) | copy-start | bytes 8752 | tf_op jit(solution)/shard_map/while
  910.6 76.9 %all-gather.3.cloned.1.call-start = ((), (), s32[]{:S(2)}) async-start(), calls=%async_computation.6 | async-start | bytes 2211840 | tf_op jit(solution)/shard_map/while/body/eval_jaxpr/all_gather | solution.py:151
  954.9 82.7 %reduce-scatter.9.cloned.1.call-start = ((), (), s32[]{:S(2)}) async-start(), calls=%async_computation.8 | async-start | bytes 2211840 | tf_op jit(solution)/shard_map/while/body/eval_jaxpr/reduce_scatter | solution.py:173
  1005.0 79.6 %all-gather.5.cloned.1.call-start = ((), (), s32[]{:S(2)}) async-start(), calls=%async_computation.9 | async-start | bytes 2211840 | tf_op jit(solution)/shard_map/while/body/eval_jaxpr/all_gather | solution.py:188
  1051.9 88.6 %reduce-scatter.7.cloned.1.call-start = ((), (), s32[]{:S(2)}) async-start(), calls=%async_computation.7 | async-start | bytes 2211840 | tf_op jit(solution)/shard_map/while/body/eval_jaxpr/reduce_scatter | solution.py:159
  1065.2 90.2 %reduce-scatter.11.cloned.1.call-start = ((), (), s32[]{:S(2)}) async-start(), calls=%async_computation.10 | async-start | bytes 2211840 | tf_op jit(solution)/shard_map/while/body/eval_jaxpr/reduce_scatter | solution.py:224
  1130.2 9.0 copy-start.25
  1146.8 19.5 %copy-start.30 = (f32[288]{0:T(512)S(1)}, f32[288]{0:T(512)}, u32[]{:S(2)}) copy-start(f32[288]{0:T(512)} %get-tuple-element.1286) | copy-start | bytes 3460 | tf_op jit(solution)/shard_map/while
  1146.8 19.5 %copy-start.33 = (f32[288]{0:T(512)S(1)}, f32[288]{0:T(512)}, u32[]{:S(2)}) copy-start(f32[288]{0:T(512)} %get-tuple-element.1285) | copy-start | bytes 3460 | tf_op jit(solution)/shard_map/while
  1155.5 13.4 copy-start.19
  1155.5 13.4 copy-start.21
  1155.5 13.4 copy-start.40
  1155.5 13.4 copy-start.42
  1171.6 172.7 %all-reduce.13.cloned.1.call-start = ((), (), s32[]{:S(2)}) async-start(), calls=%async_computation.4 | async-start | bytes 15261696 | tf_op jit(solution)/shard_map/psum | solution.py:293
  (132 other events, 667.1 us)
Sparse Core Ops, SparseCore 0:
  64.7 35.1 reduce-scatter.4
  111.8 32.4 all-gather.2
  161.9 32.4 reduce-scatter.8
  208.8 32.4 all-gather.4
  244.2 32.4 reduce-scatter.6
  279.6 32.4 reduce-scatter.10
  348.6 32.4 reduce-scatter.4
  392.9 32.4 all-gather.2
  443.0 32.4 reduce-scatter.8
  489.9 32.4 all-gather.4
  525.4 32.4 reduce-scatter.6
  560.8 32.4 reduce-scatter.10
  629.6 32.4 reduce-scatter.4
  673.9 32.4 all-gather.2
  724.0 32.4 reduce-scatter.8
  770.9 32.4 all-gather.4
  806.3 32.4 reduce-scatter.6
  841.7 32.4 reduce-scatter.10
  910.7 32.4 reduce-scatter.4
  955.0 32.4 all-gather.2
  1005.1 32.4 reduce-scatter.8
  1052.0 32.4 all-gather.4
  1087.6 32.4 reduce-scatter.6
  1123.0 32.4 reduce-scatter.10
Sparse Core Ops, SparseCore 1:
  1182.1 162.1 all-reduce.12
where the time goes:
time: 1370 us; the launch traced here: 1360 us
  waiting for transfers between devices  569 us (42%)
  matrix products  335 us (24%)
  other arithmetic  226 us (16%)
  blocking collectives  137 us (10%)
  local copies, waits for them, and re-layouts  69.1 us (5%)
  between operations  15.9 us (1%)
    psum x1, waiting for transfers between devices, local(): lax.psum(grad_qkv.astype(jnp.bfloat16), 'dp').astype(jnp.float32)  128 us
    all_gather x4, waiting for transfers between devices, layer_step(): normed_two = lax.all_gather(own_normed, 'tensor', axis=1, tiled=True)  126 us
    reduce_scatter x4, waiting for transfers between devices, layer_step(): lax.psum_scatter(back_mlp.astype(jnp.bfloat16), 'tensor', scatter_dimensi...  116 us
    reduce_scatter x4, waiting for transfers between devices, layer_step(): lax.psum_scatter(partial_out, 'tensor', scatter_dimension=1, tiled=True)  110 us
    psum x12, blocking collectives, group_stats(): return lax.psum((first, second), 'tensor')  109 us
    all_gather x4, waiting for transfers between devices, layer_step(): lax.all_gather(d_residual.astype(jnp.bfloat16), 'tensor', axis=1, tiled=T...  77.6 us
    dot_general x12, matrix products, contract_rows(): lax.dot_general(left, right, (((0,), (0,)), ((), ())), preferred_element_...  67.7 us
    dot_general x12, matrix products, contract_cols(): lax.dot_general(left, right, (((1,), (1,)), ((), ())), preferred_element_...  55.6 us
  transfers between devices with their start and end apart: 25, of which 21 were waited for; matrix products, arithmetic and copies ran while one was open for 26% of the time, Pallas kernels for 0%

commit v1 on v0

--- a/solution.py
+++ b/solution.py
@@ -290,7 +290,7 @@
     summed = (
         lax.psum(grad_gain_one.astype(jnp.bfloat16), "dp").astype(jnp.float32),
         lax.psum(grad_shift_one.astype(jnp.bfloat16), "dp").astype(jnp.float32),
-        lax.psum(grad_qkv.astype(jnp.bfloat16), "dp").astype(jnp.float32),
+        jnp.sum(lax.all_gather(grad_qkv.astype(jnp.bfloat16), "dp"), axis=0).astype(jnp.float32),
         lax.psum(grad_qv.astype(jnp.bfloat16), "dp").astype(jnp.float32),
         lax.psum(grad_out_w.astype(jnp.bfloat16), "dp").astype(jnp.float32),
         lax.psum(grad_out_b.astype(jnp.bfloat16), "dp").astype(jnp.float32),

time: 1370 us -> 1480 us (1.080)
  waiting for transfers between devices: 569 us -> 664 us
    all_gather x0 -> x1, waiting for transfers between devices: none -> 136 us  [local(): lax.all_gather(grad_qkv.astype(jnp.bfloat16), 'dp')]
    psum x1, waiting for transfers between devices: 128 us -> 86.5 us  [local(): lax.psum(grad_out_w.astype(jnp.bfloat16), 'dp').astype(jnp.float32)]
  transfers between devices with their start and end apart: 25 -> 26, of which waited for: 21 -> 22; matrix products, arithmetic and copies ran while one was open for 26% -> 25% of each run, Pallas kernels for 0% -> 0%
where the time goes in v1:
time: 1480 us; the launch traced here: 1470 us
  waiting for transfers between devices  664 us (45%)
  matrix products  334 us (23%)
  other arithmetic  238 us (16%)
  blocking collectives  137 us (9%)
  local copies, waits for them, and re-layouts  68.6 us (5%)
  between operations  15.9 us (1%)
    all_gather x1, waiting for transfers between devices, local(): lax.all_gather(grad_qkv.astype(jnp.bfloat16), 'dp')  136 us
    all_gather x4, waiting for transfers between devices, layer_step(): normed_two = lax.all_gather(own_normed, 'tensor', axis=1, tiled=True)  126 us
    reduce_scatter x4, waiting for transfers between devices, layer_step(): lax.psum_scatter(back_mlp.astype(jnp.bfloat16), 'tensor', scatter_dimensi...  116 us
    reduce_scatter x4, waiting for transfers between devices, layer_step(): lax.psum_scatter(partial_out, 'tensor', scatter_dimension=1, tiled=True)  110 us
    psum x12, blocking collectives, group_stats(): return lax.psum((first, second), 'tensor')  109 us
    psum x1, waiting for transfers between devices, local(): lax.psum(grad_out_w.astype(jnp.bfloat16), 'dp').astype(jnp.float32)  86.5 us
    all_gather x4, waiting for transfers between devices, layer_step(): lax.all_gather(d_residual.astype(jnp.bfloat16), 'tensor', axis=1, tiled=T...  77.5 us
    dot_general x12, matrix products, contract_rows(): lax.dot_general(left, right, (((0,), (0,)), ((), ())), preferred_element_...  67.7 us
  transfers between devices with their start and end apart: 26, of which 22 were waited for; matrix products, arithmetic and copies ran while one was open for 25% of the time, Pallas kernels for 0%

profile of v1, /device:TPU:0, one launch (start us, length us, event | category | flops | bytes accessed | tf_op | source)
XLA Modules:
  0.0 1469.7 jit_solution(3503463476990974221)
XLA Ops:
  16.7 12.7 copy.41
  29.4 12.7 copy.42
  42.1 1129.9 %while.42 = (s32[]{:T(128)}, f32[4,729,288]{1,2,0:T(8,128)}, f32[4,729,288]{1,2,0:T(8,128)}, f32[288]{0:T(512)}, f32[288]{0:T(512)}, /*index=5*/f32[3,1152,288]{...) while((s32[]{:T(128)}, f32[4,729,288]{1,2,0:T(8,128)}, ...), condition=%wide.region_30.31_spmd.clone, body=%wide.region_0.30_spmd.clone.sunk | while | flops 18614964224 | bytes 394633504 | solution.py:273
  70.5 29.5 %reduce-scatter.5.cloned.1.call-done = bf16[729,288]{0,1:T(8,128)(2,1)} async-done(((bf16[729,1152]{0,1:T(8,128)(2,1)}), bf16[729,288]{0,1:T(8,128)(2,1)}) %reduce-scatter.5.cloned.1.call-update) | async-done | bytes 419920 | tf_op jit(solution)/shard_map/while/body/eval_jaxpr/reduce_scatter | solution.py:137
  101.5 9.1 all-reduce.8
  112.9 31.3 %all-gather.7.cloned.1.call-done = bf16[729,1152]{0,1:T(8,128)(2,1)} async-done(((bf16[729,288]{0,1:T(8,128)(2,1)}), bf16[729,1152]{0,1:T(8,128)(2,1)}) %all-gather.7.cloned.1.call-update) | async-done | bytes 1679632 | tf_op jit(solution)/shard_map/while/body/eval_jaxpr/all_gather | solution.py:151
  148.9 7.7 convert_reduce_fusion.11
  165.3 29.0 %reduce-scatter.9.cloned.1.call-done = bf16[729,288]{0,1:T(8,128)(2,1)} async-done(((bf16[729,1152]{0,1:T(8,128)(2,1)}), bf16[729,288]{0,1:T(8,128)(2,1)}) %reduce-scatter.9.cloned.1.call-update) | async-done | bytes 419920 | tf_op jit(solution)/shard_map/while/body/eval_jaxpr/reduce_scatter | solution.py:173
  196.3 9.1 all-reduce.9
  215.2 6.1 convolution_convert_fusion.17
  221.4 19.9 %all-gather.9.cloned.1.call-done = bf16[729,1152]{0,1:T(8,128)(2,1)} async-done(((bf16[729,288]{0,1:T(8,128)(2,1)}), bf16[729,1152]{0,1:T(8,128)(2,1)}) %all-gather.9.cloned.1.call-update) | async-done | bytes 1679632 | tf_op jit(solution)/shard_map/while/body/eval_jaxpr/all_gather | solution.py:188
  243.6 7.6 multiply_reduce_fusion.9
  251.2 10.4 multiply_convert_fusion.9
  278.1 6.8 convolution_add_fusion.12
  285.5 6.8 convolution_add_fusion.13
  299.2 6.0 bitcast_add_fusion.3
  305.1 6.9 reduce-scatter.11.cloned.1.call-done
  313.7 9.1 all-reduce.10
  354.3 26.8 %reduce-scatter.5.cloned.1.call-done = bf16[729,288]{0,1:T(8,128)(2,1)} async-done(((bf16[729,1152]{0,1:T(8,128)(2,1)}), bf16[729,288]{0,1:T(8,128)(2,1)}) %reduce-scatter.5.cloned.1.call-update) | async-done | bytes 419920 | tf_op jit(solution)/shard_map/while/body/eval_jaxpr/reduce_scatter | solution.py:137
  382.6 9.1 all-reduce.8
  393.6 31.7 %all-gather.7.cloned.1.call-done = bf16[729,1152]{0,1:T(8,128)(2,1)} async-done(((bf16[729,288]{0,1:T(8,128)(2,1)}), bf16[729,1152]{0,1:T(8,128)(2,1)}) %all-gather.7.cloned.1.call-update) | async-done | bytes 1679632 | tf_op jit(solution)/shard_map/while/body/eval_jaxpr/all_gather | solution.py:151
  430.0 7.7 convert_reduce_fusion.11
  446.4 29.0 %reduce-scatter.9.cloned.1.call-done = bf16[729,288]{0,1:T(8,128)(2,1)} async-done(((bf16[729,1152]{0,1:T(8,128)(2,1)}), bf16[729,288]{0,1:T(8,128)(2,1)}) %reduce-scatter.9.cloned.1.call-update) | async-done | bytes 419920 | tf_op jit(solution)/shard_map/while/body/eval_jaxpr/reduce_scatter | solution.py:173
  477.4 9.1 all-reduce.9
  496.9 6.1 convolution_convert_fusion.17
  503.1 19.2 %all-gather.9.cloned.1.call-done = bf16[729,1152]{0,1:T(8,128)(2,1)} async-done(((bf16[729,288]{0,1:T(8,128)(2,1)}), bf16[729,1152]{0,1:T(8,128)(2,1)}) %all-gather.9.cloned.1.call-update) | async-done | bytes 1679632 | tf_op jit(solution)/shard_map/while/body/eval_jaxpr/all_gather | solution.py:188
  524.7 7.6 multiply_reduce_fusion.9
  532.3 10.3 multiply_convert_fusion.9
  559.2 8.2 convolution_add_fusion.12
  568.1 8.4 convolution_add_fusion.13
  584.6 7.2 bitcast_add_fusion.3
  595.0 9.1 all-reduce.10
  635.3 26.8 %reduce-scatter.5.cloned.1.call-done = bf16[729,288]{0,1:T(8,128)(2,1)} async-done(((bf16[729,1152]{0,1:T(8,128)(2,1)}), bf16[729,288]{0,1:T(8,128)(2,1)}) %reduce-scatter.5.cloned.1.call-update) | async-done | bytes 419920 | tf_op jit(solution)/shard_map/while/body/eval_jaxpr/reduce_scatter | solution.py:137
  663.6 9.1 all-reduce.8
  674.8 31.5 %all-gather.7.cloned.1.call-done = bf16[729,1152]{0,1:T(8,128)(2,1)} async-done(((bf16[729,288]{0,1:T(8,128)(2,1)}), bf16[729,1152]{0,1:T(8,128)(2,1)}) %all-gather.7.cloned.1.call-update) | async-done | bytes 1679632 | tf_op jit(solution)/shard_map/while/body/eval_jaxpr/all_gather | solution.py:151
  711.0 7.7 convert_reduce_fusion.11
  727.4 29.0 %reduce-scatter.9.cloned.1.call-done = bf16[729,288]{0,1:T(8,128)(2,1)} async-done(((bf16[729,1152]{0,1:T(8,128)(2,1)}), bf16[729,288]{0,1:T(8,128)(2,1)}) %reduce-scatter.9.cloned.1.call-update) | async-done | bytes 419920 | tf_op jit(solution)/shard_map/while/body/eval_jaxpr/reduce_scatter | solution.py:173
  758.4 9.1 all-reduce.9
  777.9 6.1 convolution_convert_fusion.17
  784.1 19.2 %all-gather.9.cloned.1.call-done = bf16[729,1152]{0,1:T(8,128)(2,1)} async-done(((bf16[729,288]{0,1:T(8,128)(2,1)}), bf16[729,1152]{0,1:T(8,128)(2,1)}) %all-gather.9.cloned.1.call-update) | async-done | bytes 1679632 | tf_op jit(solution)/shard_map/while/body/eval_jaxpr/all_gather | solution.py:188
  805.7 7.6 multiply_reduce_fusion.9
  813.3 10.4 multiply_convert_fusion.9
  840.2 8.2 convolution_add_fusion.12
  849.1 8.2 convolution_add_fusion.13
  865.4 7.2 bitcast_add_fusion.3
  875.8 9.1 all-reduce.10
  916.4 26.8 %reduce-scatter.5.cloned.1.call-done = bf16[729,288]{0,1:T(8,128)(2,1)} async-done(((bf16[729,1152]{0,1:T(8,128)(2,1)}), bf16[729,288]{0,1:T(8,128)(2,1)}) %reduce-scatter.5.cloned.1.call-update) | async-done | bytes 419920 | tf_op jit(solution)/shard_map/while/body/eval_jaxpr/reduce_scatter | solution.py:137
  944.7 9.1 all-reduce.8
  955.6 31.7 %all-gather.7.cloned.1.call-done = bf16[729,1152]{0,1:T(8,128)(2,1)} async-done(((bf16[729,288]{0,1:T(8,128)(2,1)}), bf16[729,1152]{0,1:T(8,128)(2,1)}) %all-gather.7.cloned.1.call-update) | async-done | bytes 1679632 | tf_op jit(solution)/shard_map/while/body/eval_jaxpr/all_gather | solution.py:151
  992.1 7.7 convert_reduce_fusion.11
  1008.5 29.0 %reduce-scatter.9.cloned.1.call-done = bf16[729,288]{0,1:T(8,128)(2,1)} async-done(((bf16[729,1152]{0,1:T(8,128)(2,1)}), bf16[729,288]{0,1:T(8,128)(2,1)}) %reduce-scatter.9.cloned.1.call-update) | async-done | bytes 419920 | tf_op jit(solution)/shard_map/while/body/eval_jaxpr/reduce_scatter | solution.py:173
  1039.5 9.0 all-reduce.9
  1059.0 6.1 convolution_convert_fusion.17
  1065.2 19.2 %all-gather.9.cloned.1.call-done = bf16[729,1152]{0,1:T(8,128)(2,1)} async-done(((bf16[729,288]{0,1:T(8,128)(2,1)}), bf16[729,1152]{0,1:T(8,128)(2,1)}) %all-gather.9.cloned.1.call-update) | async-done | bytes 1679632 | tf_op jit(solution)/shard_map/while/body/eval_jaxpr/all_gather | solution.py:188
  1086.8 7.6 multiply_reduce_fusion.9
  1094.4 10.3 multiply_convert_fusion.9
  1121.3 8.2 convolution_add_fusion.12
  1130.2 8.4 convolution_add_fusion.13
  1146.7 7.2 bitcast_add_fusion.3
  1157.1 9.1 all-reduce.10
  1186.2 28.1 %all-reduce.3 = (bf16[288]{0:T(512)(128)(2,1)S(1)}, bf16[288]{0:T(512)(128)(2,1)S(1)}, bf16[2,288]{1,0:T(2,128)(2,1)S(1)}, bf16[288]{0:T(512)(128)(2,1)S(1)}, bf...) all-reduce(bf16[288]{0:T(512)(128)(2,1)S(1)} %convert_element_type., ...), channel_id=1, replica_groups=mesh['tensor'=4,'dp'=8] {'dp'}, use_global_device_ids=true, to_apply=%region_31.32 | all-reduce | flops 3380 | bytes 13520 | tf_op jit(solution)/shard_map/psum | solution.py:291
  1219.0 86.5 %all-reduce.13.cloned.1.call-done = (bf16[288,1152]{1,0:T(8,128)(2,1)}, bf16[1152,1076]{0,1:T(8,128)(2,1)}, bf16[1076,1152]{1,0:T(8,128)(2,1)}) async-done(((bf16[288,1152]{1,0:T(8,128)(2,1)}, bf16[1152,1076]{0,1:T(8,128)(2,1)}, bf16[1076,1152]{1,0:T(8,128)(2,1)}), (bf16[288,1152]{1,0:T(8,128)(2,1)}, bf16[1152,1076]{0,1:T(8,128)(2,1)}, bf16[1076,1152]{1,0:T(8,128)(2,1)})) %all-reduce.13.cloned.1.call-update) | async-done | bytes 5621776 | tf_op jit(solution)/shard_map/psum | solution.py:295
  1314.8 135.8 %all-gather.5.cloned.1.call-done = bf16[24,1152,288]{1,2,0:T(8,128)(2,1)} async-done(((bf16[3,1152,288]{1,2,0:T(8,128)(2,1)}), bf16[24,1152,288]{1,2,0:T(8,128)(2,1)}) %all-gather.5.cloned.1.call-update) | async-done | bytes 15925264 | tf_op jit(solution)/shard_map/all_gather | solution.py:293
  1450.7 9.2 reduce_sum.300
  (635 shorter events, 396.3 us)
Async XLA Ops:
  42.1 9.8 copy-start.39
  42.1 166.6 %copy-start.16 = (f32[1152]{0:T(1024)}, f32[1152]{0:T(1024)S(1)}, u32[]{:S(2)}) copy-start(f32[1152]{0:T(1024)S(1)} %get-tuple-element.1364) | copy-start | bytes 13828 | tf_op jit(solution)/shard_map/while
  42.1 57.8 %reduce-scatter.5.cloned.1.call-start = ((), (), s32[]{:S(2)}) async-start(), calls=%async_computation.6 | async-start | bytes 2211840 | tf_op jit(solution)/shard_map/while/body/eval_jaxpr/reduce_scatter | solution.py:137
  44.0 167.6 %copy-start.13 = (f32[729]{0:T(1024)}, f32[729]{0:T(1024)S(1)}, u32[]{:S(2)}) copy-start(f32[729]{0:T(1024)S(1)} %broadcast_multiply_fusion.11) | copy-start | bytes 8752 | tf_op jit(solution)/shard_map/while
  64.6 79.6 %all-gather.7.cloned.1.call-start = ((), (), s32[]{:S(2)}) async-start(), calls=%async_computation.7 | async-start | bytes 2211840 | tf_op jit(solution)/shard_map/while/body/eval_jaxpr/all_gather | solution.py:151
  111.6 82.7 %reduce-scatter.9.cloned.1.call-start = ((), (), s32[]{:S(2)}) async-start(), calls=%async_computation.9 | async-start | bytes 2211840 | tf_op jit(solution)/shard_map/while/body/eval_jaxpr/reduce_scatter | solution.py:173
  161.7 79.5 %all-gather.9.cloned.1.call-start = ((), (), s32[]{:S(2)}) async-start(), calls=%async_computation.10 | async-start | bytes 2211840 | tf_op jit(solution)/shard_map/while/body/eval_jaxpr/all_gather | solution.py:188
  208.6 84.9 %reduce-scatter.7.cloned.1.call-start = ((), (), s32[]{:S(2)}) async-start(), calls=%async_computation.8 | async-start | bytes 2211840 | tf_op jit(solution)/shard_map/while/body/eval_jaxpr/reduce_scatter | solution.py:159
  221.3 90.7 %reduce-scatter.11.cloned.1.call-start = ((), (), s32[]{:S(2)}) async-start(), calls=%async_computation.11 | async-start | bytes 2211840 | tf_op jit(solution)/shard_map/while/body/eval_jaxpr/reduce_scatter | solution.py:224
  299.1 12.9 copy-start.15
  299.2 23.7 %copy-start.28 = (f32[288]{0:T(512)S(1)}, f32[288]{0:T(512)}, u32[]{:S(2)}) copy-start(f32[288]{0:T(512)} %get-tuple-element.1316) | copy-start | bytes 3460 | tf_op jit(solution)/shard_map/while
  299.2 23.7 %copy-start.31 = (f32[288]{0:T(512)S(1)}, f32[288]{0:T(512)}, u32[]{:S(2)}) copy-start(f32[288]{0:T(512)} %get-tuple-element.1315) | copy-start | bytes 3460 | tf_op jit(solution)/shard_map/while
  312.0 13.4 copy-start.17
  312.0 13.4 copy-start.19
  312.0 13.4 copy-start.38
  312.0 13.4 copy-start.40
  325.9 9.8 copy-start.39
  325.9 163.9 %copy-start.16 = (f32[1152]{0:T(1024)}, f32[1152]{0:T(1024)S(1)}, u32[]{:S(2)}) copy-start(f32[1152]{0:T(1024)S(1)} %get-tuple-element.1364) | copy-start | bytes 13828 | tf_op jit(solution)/shard_map/while
  325.9 55.1 %reduce-scatter.5.cloned.1.call-start = ((), (), s32[]{:S(2)}) async-start(), calls=%async_computation.6 | async-start | bytes 2211840 | tf_op jit(solution)/shard_map/while/body/eval_jaxpr/reduce_scatter | solution.py:137
  327.8 165.5 %copy-start.13 = (f32[729]{0:T(1024)}, f32[729]{0:T(1024)S(1)}, u32[]{:S(2)}) copy-start(f32[729]{0:T(1024)S(1)} %broadcast_multiply_fusion.11) | copy-start | bytes 8752 | tf_op jit(solution)/shard_map/while
  348.4 76.9 %all-gather.7.cloned.1.call-start = ((), (), s32[]{:S(2)}) async-start(), calls=%async_computation.7 | async-start | bytes 2211840 | tf_op jit(solution)/shard_map/while/body/eval_jaxpr/all_gather | solution.py:151
  392.7 82.7 %reduce-scatter.9.cloned.1.call-start = ((), (), s32[]{:S(2)}) async-start(), calls=%async_computation.9 | async-start | bytes 2211840 | tf_op jit(solution)/shard_map/while/body/eval_jaxpr/reduce_scatter | solution.py:173
  442.8 79.5 %all-gather.9.cloned.1.call-start = ((), (), s32[]{:S(2)}) async-start(), calls=%async_computation.10 | async-start | bytes 2211840 | tf_op jit(solution)/shard_map/while/body/eval_jaxpr/all_gather | solution.py:188
  489.7 88.6 %reduce-scatter.7.cloned.1.call-start = ((), (), s32[]{:S(2)}) async-start(), calls=%async_computation.8 | async-start | bytes 2211840 | tf_op jit(solution)/shard_map/while/body/eval_jaxpr/reduce_scatter | solution.py:159
  503.1 90.2 %reduce-scatter.11.cloned.1.call-start = ((), (), s32[]{:S(2)}) async-start(), calls=%async_computation.11 | async-start | bytes 2211840 | tf_op jit(solution)/shard_map/while/body/eval_jaxpr/reduce_scatter | solution.py:224
  568.1 9.0 copy-start.23
  584.6 19.5 %copy-start.28 = (f32[288]{0:T(512)S(1)}, f32[288]{0:T(512)}, u32[]{:S(2)}) copy-start(f32[288]{0:T(512)} %get-tuple-element.1316) | copy-start | bytes 3460 | tf_op jit(solution)/shard_map/while
  584.6 19.5 %copy-start.31 = (f32[288]{0:T(512)S(1)}, f32[288]{0:T(512)}, u32[]{:S(2)}) copy-start(f32[288]{0:T(512)} %get-tuple-element.1315) | copy-start | bytes 3460 | tf_op jit(solution)/shard_map/while
  593.3 13.4 copy-start.17
  593.3 13.4 copy-start.19
  593.3 13.4 copy-start.38
  593.3 13.4 copy-start.40
  606.9 9.8 copy-start.39
  606.9 163.9 %copy-start.16 = (f32[1152]{0:T(1024)}, f32[1152]{0:T(1024)S(1)}, u32[]{:S(2)}) copy-start(f32[1152]{0:T(1024)S(1)} %get-tuple-element.1364) | copy-start | bytes 13828 | tf_op jit(solution)/shard_map/while
  606.9 55.1 %reduce-scatter.5.cloned.1.call-start = ((), (), s32[]{:S(2)}) async-start(), calls=%async_computation.6 | async-start | bytes 2211840 | tf_op jit(solution)/shard_map/while/body/eval_jaxpr/reduce_scatter | solution.py:137
  608.8 165.5 %copy-start.13 = (f32[729]{0:T(1024)}, f32[729]{0:T(1024)S(1)}, u32[]{:S(2)}) copy-start(f32[729]{0:T(1024)S(1)} %broadcast_multiply_fusion.11) | copy-start | bytes 8752 | tf_op jit(solution)/shard_map/while
  629.4 76.9 %all-gather.7.cloned.1.call-start = ((), (), s32[]{:S(2)}) async-start(), calls=%async_computation.7 | async-start | bytes 2211840 | tf_op jit(solution)/shard_map/while/body/eval_jaxpr/all_gather | solution.py:151
  673.7 82.7 %reduce-scatter.9.cloned.1.call-start = ((), (), s32[]{:S(2)}) async-start(), calls=%async_computation.9 | async-start | bytes 2211840 | tf_op jit(solution)/shard_map/while/body/eval_jaxpr/reduce_scatter | solution.py:173
  723.8 79.5 %all-gather.9.cloned.1.call-start = ((), (), s32[]{:S(2)}) async-start(), calls=%async_computation.10 | async-start | bytes 2211840 | tf_op jit(solution)/shard_map/while/body/eval_jaxpr/all_gather | solution.py:188
  770.7 88.5 %reduce-scatter.7.cloned.1.call-start = ((), (), s32[]{:S(2)}) async-start(), calls=%async_computation.8 | async-start | bytes 2211840 | tf_op jit(solution)/shard_map/while/body/eval_jaxpr/reduce_scatter | solution.py:159
  784.1 90.0 %reduce-scatter.11.cloned.1.call-start = ((), (), s32[]{:S(2)}) async-start(), calls=%async_computation.11 | async-start | bytes 2211840 | tf_op jit(solution)/shard_map/while/body/eval_jaxpr/reduce_scatter | solution.py:224
  865.4 19.5 %copy-start.28 = (f32[288]{0:T(512)S(1)}, f32[288]{0:T(512)}, u32[]{:S(2)}) copy-start(f32[288]{0:T(512)} %get-tuple-element.1316) | copy-start | bytes 3460 | tf_op jit(solution)/shard_map/while
  865.4 19.5 %copy-start.31 = (f32[288]{0:T(512)S(1)}, f32[288]{0:T(512)}, u32[]{:S(2)}) copy-start(f32[288]{0:T(512)} %get-tuple-element.1315) | copy-start | bytes 3460 | tf_op jit(solution)/shard_map/while
  874.1 13.4 copy-start.17
  874.1 13.4 copy-start.19
  874.1 13.4 copy-start.38
  874.1 13.4 copy-start.40
  888.0 9.8 copy-start.39
  888.0 163.9 %copy-start.16 = (f32[1152]{0:T(1024)}, f32[1152]{0:T(1024)S(1)}, u32[]{:S(2)}) copy-start(f32[1152]{0:T(1024)S(1)} %get-tuple-element.1364) | copy-start | bytes 13828 | tf_op jit(solution)/shard_map/while
  888.0 55.1 %reduce-scatter.5.cloned.1.call-start = ((), (), s32[]{:S(2)}) async-start(), calls=%async_computation.6 | async-start | bytes 2211840 | tf_op jit(solution)/shard_map/while/body/eval_jaxpr/reduce_scatter | solution.py:137
  889.9 165.5 %copy-start.13 = (f32[729]{0:T(1024)}, f32[729]{0:T(1024)S(1)}, u32[]{:S(2)}) copy-start(f32[729]{0:T(1024)S(1)} %broadcast_multiply_fusion.11) | copy-start | bytes 8752 | tf_op jit(solution)/shard_map/while
  910.5 76.9 %all-gather.7.cloned.1.call-start = ((), (), s32[]{:S(2)}) async-start(), calls=%async_computation.7 | async-start | bytes 2211840 | tf_op jit(solution)/shard_map/while/body/eval_jaxpr/all_gather | solution.py:151
  954.8 82.7 %reduce-scatter.9.cloned.1.call-start = ((), (), s32[]{:S(2)}) async-start(), calls=%async_computation.9 | async-start | bytes 2211840 | tf_op jit(solution)/shard_map/while/body/eval_jaxpr/reduce_scatter | solution.py:173
  1004.9 79.5 %all-gather.9.cloned.1.call-start = ((), (), s32[]{:S(2)}) async-start(), calls=%async_computation.10 | async-start | bytes 2211840 | tf_op jit(solution)/shard_map/while/body/eval_jaxpr/all_gather | solution.py:188
  1051.8 88.7 %reduce-scatter.7.cloned.1.call-start = ((), (), s32[]{:S(2)}) async-start(), calls=%async_computation.8 | async-start | bytes 2211840 | tf_op jit(solution)/shard_map/while/body/eval_jaxpr/reduce_scatter | solution.py:159
  1065.1 90.2 %reduce-scatter.11.cloned.1.call-start = ((), (), s32[]{:S(2)}) async-start(), calls=%async_computation.11 | async-start | bytes 2211840 | tf_op jit(solution)/shard_map/while/body/eval_jaxpr/reduce_scatter | solution.py:224
  1146.7 19.5 %copy-start.28 = (f32[288]{0:T(512)S(1)}, f32[288]{0:T(512)}, u32[]{:S(2)}) copy-start(f32[288]{0:T(512)} %get-tuple-element.1316) | copy-start | bytes 3460 | tf_op jit(solution)/shard_map/while
  1146.7 19.5 %copy-start.31 = (f32[288]{0:T(512)S(1)}, f32[288]{0:T(512)}, u32[]{:S(2)}) copy-start(f32[288]{0:T(512)} %get-tuple-element.1315) | copy-start | bytes 3460 | tf_op jit(solution)/shard_map/while
  1155.4 13.4 copy-start.17
  1155.4 13.4 copy-start.19
  1155.4 13.4 copy-start.38
  1155.4 13.4 copy-start.40
  1172.0 133.5 %all-reduce.13.cloned.1.call-start = ((), (), s32[]{:S(2)}) async-start(), calls=%async_computation.5 | async-start | bytes 11280384 | tf_op jit(solution)/shard_map/psum | solution.py:295
  1180.3 270.4 %all-gather.5.cloned.1.call-start = ((), (), s32[]{:S(2)}) async-start(), calls=%async_computation.4 | async-start | bytes 17915904 | tf_op jit(solution)/shard_map/all_gather | solution.py:293
  (129 other events, 673.6 us)
Sparse Core Ops, SparseCore 0:
  64.7 35.1 reduce-scatter.4
  111.7 32.4 all-gather.6
  161.8 32.4 reduce-scatter.8
  208.8 32.4 all-gather.8
  244.1 32.4 reduce-scatter.6
  279.5 32.4 reduce-scatter.10
  348.5 32.4 reduce-scatter.4
  392.8 32.4 all-gather.6
  442.9 32.4 reduce-scatter.8
  489.8 32.4 all-gather.8
  525.3 32.4 reduce-scatter.6
  560.8 32.4 reduce-scatter.10
  629.5 32.4 reduce-scatter.4
  673.8 32.4 all-gather.6
  723.9 32.4 reduce-scatter.8
  770.8 32.4 all-gather.8
  806.2 32.4 reduce-scatter.6
  841.6 32.4 reduce-scatter.10
  910.6 32.4 reduce-scatter.4
  954.9 32.4 all-gather.6
  1005.0 32.4 reduce-scatter.8
  1051.9 32.4 all-gather.8
  1087.4 32.4 reduce-scatter.6
  1122.8 32.4 reduce-scatter.10
Sparse Core Ops, SparseCore 1:
  1180.4 125.0 all-reduce.12
  1307.0 143.7 all-gather.4
